TPU v7x, 32 devices: a whole 2x2x4 slice. The times are simulated.
32 devices in a mesh: blk: 16 (over z, y, core), head: 2 (over x).
Axes of the slice: x: 2, y: 2, z: 4, core: 2. Of those that a mesh axis runs over, the one named last changes fastest.
Arguments:
- query_nope: bfloat16 [1024, 8192], P('blk', 'head'), may hold values from -140 to 140
- query_rope: bfloat16 [1024, 4096], P('blk', 'head'), may hold values from -6 to 6
- compressed: bfloat16 [1024, 576], P(('blk', 'head')), may hold values from -6 to 6
- latent_gain: float32 [512], replicated, may hold values from 0.1 to 1.9
- key_up: bfloat16 [64, 128, 512], P('head'), may hold values from -0.5 to 0.5
- value_up: bfloat16 [64, 512, 128], P('head'), may hold values from -1.5 to 1.5
- span_order: int32 [32], replicated, may hold values from 0 to 31, each once
Outputs:
- attended: bfloat16 [1024, 8192], P('blk', 'head')
Inputs may be any that keep to these rules, and one draw needn't show every extreme that they name: Every number appears once; device index i of blk holds the blocks span_order[2 i] and span_order[2 i + 1].
All inputs are finite; a program needn't handle non-finite values.
Results may differ from a plain program's by a relative error of at most 0.0075.
The roundings to bfloat16 on the way count: a program that leaves them out, or rounds other values in their place, can miss the bound.
Values may be sent and summed in bfloat16 or wider, within the bound.
A program may use at most 64 MiB of HBM per device.

v0:
```python
import functools
import math

import jax
import jax.numpy as jnp
import numpy as np
from jax import lax
from jax.experimental import pallas as pl
from jax.experimental.pallas import tpu as pltpu
from jax.sharding import PartitionSpec as P

norm_epsilon = 1e-06
rope_base = 10000.0
masked_score = -1e30
LANES = 128
GROUP = 16
MESH = pl.DeviceIdType.MESH


def rotate_tile(tile, cosine, signed_sine, rope_width):
    half = rope_width // 2
    width = tile.shape[-1]
    lane = lax.broadcasted_iota(jnp.int32, tile.shape, 1)
    partner = jnp.where(
        lane % rope_width < half,
        pltpu.roll(tile, width - half, 1),
        pltpu.roll(tile, half, 1),
    )
    return tile * cosine + partner * signed_sine


def angles_of(positions, freq, rope_width):
    angles = positions.astype(jnp.float32) * freq
    lane = lax.broadcasted_iota(jnp.int32, angles.shape, 1)
    sine = jnp.sin(angles)
    return jnp.cos(angles), jnp.where(lane % rope_width < rope_width // 2, -sine, sine)


def body(
    dims,
    remote,
    span_ref,
    keys_in_ref,
    gain_ref,
    freq_ref,
    nope_hbm,
    rope_hbm,
    key_up_hbm,
    value_up_hbm,
    out_hbm,
    nope_ref,
    rope_ref,
    key_up_ref,
    value_up_ref,
    out_ref,
    keys_ref,
    query_ref,
    mask_ref,
    load_sem,
    out_sem,
    send_sem,
    recv_sem,
):
    tokens, heads, nope, latent, rope, value, total, slices = dims
    half_block = tokens // 2
    scale = (nope + rope) ** (-0.5) * math.log2(math.e)
    blk = lax.axis_index("blk")
    head = lax.axis_index("head")
    loads = [
        pltpu.make_async_copy(nope_hbm, nope_ref, load_sem.at[0]),
        pltpu.make_async_copy(rope_hbm, rope_ref, load_sem.at[1]),
        pltpu.make_async_copy(key_up_hbm, key_up_ref, load_sem.at[2]),
        pltpu.make_async_copy(value_up_hbm, value_up_ref, load_sem.at[3]),
    ]
    for load in loads:
        load.start()

    sends = []
    if remote:
        outer = lax.axis_size("blk") // 4
        o, i, c = blk // 4, (blk // 2) % 2, blk % 2

        def device(o_, i_, c_, h_):
            return ((o_ * 2 + i_) * 2 + c_, h_)

        def slot(o_, i_, c_, h_):
            return ((o_ * 2 + i_) * 2 + c_) * 2 + h_

        def block_at(index):
            return keys_ref.at[pl.ds(pl.multiple_of(index * slices, slices), slices)]

        def send(index, target):
            copy = pltpu.make_async_remote_copy(
                src_ref=block_at(index),
                dst_ref=block_at(index),
                send_sem=send_sem.at[len(sends)],
                recv_sem=recv_sem.at[index],
                device_id=target,
                device_id_type=MESH,
            )
            copy.start()
            sends.append(copy)

        def arrive(index):
            pltpu.make_async_remote_copy(
                src_ref=block_at(index),
                dst_ref=block_at(index),
                send_sem=send_sem.at[0],
                recv_sem=recv_sem.at[index],
                device_id=device(o, i, 1 - c, head),
                device_id_type=MESH,
            ).wait_recv()

        sibling = device(o, i, 1 - c, head)
        i_peer = device(o, 1 - i, c, head)
        h_peer = device(o, i, c, 1 - head)
        order = []
        for d in range(1, outer // 2 + 1):
            order.append(d)
            if d != outer - d:
                order.append(outer - d)
        at = lambda d: lax.rem(o + d, outer)
        o_peers = [device(at(d), i, c, head) for d in order]
        peers = [sibling, i_peer, h_peer] + o_peers
        barrier = pltpu.get_barrier_semaphore()
        for peer in peers:
            pl.semaphore_signal(barrier, inc=1, device_id=peer, device_id_type=MESH)

        first_row = blk * tokens + head * slices
        own_pos = (
            span_ref[first_row // half_block] * half_block
            + first_row % half_block
            + lax.broadcasted_iota(jnp.int32, (slices, LANES), 0)
        )
        own = keys_in_ref[...].astype(jnp.float32)
        own_latent = own[:, :latent]
        own_latent = (
            own_latent
            * lax.rsqrt(jnp.mean(own_latent * own_latent, axis=1, keepdims=True) + norm_epsilon)
            * gain_ref[...]
        )
        cosine, sine = angles_of(own_pos, freq_ref[...], rope)
        own_rope = own[:, latent : latent + rope]
        own_rope = jnp.concatenate([own_rope] * (LANES // rope), axis=1)
        own_slot = slot(o, i, c, head)
        own_block = block_at(own_slot)
        own_block[:, :latent] = own_latent.astype(jnp.bfloat16)
        own_block[:, latent:] = rotate_tile(own_rope, cosine, sine, rope).astype(jnp.bfloat16)

        pl.semaphore_wait(barrier, len(peers))
        for peer in [i_peer, h_peer] + o_peers + [sibling]:
            send(own_slot, peer)
    else:
        keys_copy = pltpu.make_async_copy(keys_in_ref, keys_ref, load_sem.at[4])
        keys_copy.start()

    token = lax.broadcasted_iota(jnp.int32, (tokens, LANES), 0)
    query_pos = (
        jnp.where(token < half_block, span_ref[blk * 2], span_ref[blk * 2 + 1]) * half_block
        + token % half_block
    )
    key_lane = lax.broadcasted_iota(jnp.int32, (8, total), 1)
    key_half = key_lane // half_block
    key_span = jnp.zeros((8, total), jnp.int32)
    for entry in range(total // half_block):
        key_span = jnp.where(key_half == entry, span_ref[entry], key_span)
    key_pos = key_span * half_block + key_lane % half_block
    mask_ref[...] = jnp.where(key_pos[:1] <= query_pos[:, :1], 0.0, masked_score)
    cosine, sine = angles_of(query_pos, freq_ref[...], rope)
    loads[1].wait()
    per_tile = LANES // rope
    lane = lax.broadcasted_iota(jnp.int32, (tokens, LANES), 1)
    for tile in range(heads // per_tile):
        columns = rope_ref[:, tile * LANES : (tile + 1) * LANES].astype(jnp.float32)
        rotated = rotate_tile(columns, cosine, sine, rope)
        for part in range(per_tile):
            row = (tile * per_tile + part) * tokens
            query_ref[row : row + tokens, latent:] = jnp.where(
                lane // rope == part, rotated, 0.0
            ).astype(jnp.bfloat16)

    if remote:
        for d in order:
            index = slot(at(d), i, c, head)
            arrive(index)
            for peer in (i_peer, h_peer, sibling):
                send(index, peer)

    loads[0].wait()
    loads[2].wait()

    def lift(first, count):
        for h in range(first, first + count):
            query_ref[h * tokens : (h + 1) * tokens, :latent] = jnp.dot(
                nope_ref[:, h * nope : (h + 1) * nope],
                key_up_ref[h],
                preferred_element_type=jnp.float32,
            ).astype(jnp.bfloat16)

    if remote:
        steps = [0] + order
        per_step = -(-heads // len(steps))
        for n, d in enumerate(steps):
            lift(n * per_step, max(0, min(per_step, heads - n * per_step)))
            via_h, via_i = slot(at(d), i, c, 1 - head), slot(at(d), 1 - i, c, head)
            arrive(via_i)
            if d % 2 == 1:
                send(via_i, h_peer)
            send(via_i, sibling)
            arrive(via_h)
            if d % 2 == 0:
                send(via_h, i_peer)
            send(via_h, sibling)
        for d in steps:
            index = slot(at(d), 1 - i, c, 1 - head)
            arrive(index)
            send(index, sibling)
        for d in steps:
            for i_ in (i, 1 - i):
                for h_ in (head, 1 - head):
                    arrive(slot(at(d), i_, 1 - c, h_))
    else:
        lift(0, heads)
        keys_copy.wait()
    loads[3].wait()

    group = min(GROUP, heads)
    rows = group * tokens

    def attend(g, _):
        start = pl.multiple_of(g * rows, rows)
        scores = lax.dot_general(
            query_ref[pl.ds(start, rows), :],
            keys_ref[...],
            (((1,), (1,)), ((), ())),
            preferred_element_type=jnp.float32,
        )
        scores = scores.reshape(group, tokens, total) + mask_ref[...][None]
        top = jnp.max(scores, axis=2, keepdims=True)
        weight = jnp.exp2((scores - top) * scale)
        sums = jnp.sum(weight, axis=2, keepdims=True).reshape(rows, 1)
        product = jnp.dot(
            weight.reshape(rows, total).astype(jnp.bfloat16),
            keys_ref[:, :latent],
            preferred_element_type=jnp.float32,
        )
        lat_out = (product * (1.0 / sums)).astype(jnp.bfloat16)
        for n in range(group):
            column = pl.multiple_of((g * group + n) * value, value)
            out_ref[:, pl.ds(column, value)] = jnp.dot(
                lat_out[n * tokens : (n + 1) * tokens],
                value_up_ref[g * group + n],
                preferred_element_type=jnp.float32,
            ).astype(jnp.bfloat16)
        return 0

    lax.fori_loop(0, heads // group, attend, 0)
    store = pltpu.make_async_copy(out_ref, out_hbm, out_sem.at[0])
    store.start()
    for copy in sends:
        copy.wait_send()
    store.wait()


def shards(
    mesh, query_nope, query_rope, compressed, latent_gain, key_up, value_up, span_order
):
    tokens, (heads, nope, latent) = query_nope.shape[0], key_up.shape
    rope, value = query_rope.shape[1] // heads, value_up.shape[2]
    slices = compressed.shape[0]
    blocks, head_parts = mesh.shape["blk"], mesh.shape["head"]
    total = blocks * tokens
    half_block = tokens // 2
    half = rope // 2
    remote = head_parts == 2 and blocks % 4 == 0 and slices % 16 == 0 and half_block % slices == 0
    exponents = np.arange(LANES) % half
    freq = jnp.asarray((rope_base ** (-exponents / half)).astype(np.float32))[None]
    gain = latent_gain[None]
    if remote:
        keys_in = compressed
    else:
        rows = (
            lax.axis_index("blk") * tokens
            + lax.axis_index("head") * slices
            + jnp.arange(slices, dtype=jnp.int32)
        )
        pos = span_order[rows // half_block] * half_block + rows % half_block
        wide = compressed.astype(jnp.float32)
        lat = wide[:, :latent]
        lat = lat * lax.rsqrt(jnp.mean(lat * lat, axis=1, keepdims=True) + norm_epsilon) * gain
        angles = pos.astype(jnp.float32)[:, None] * freq[:, :half]
        a, b = wide[:, latent : latent + half], wide[:, latent + half :]
        cosine, sine = jnp.cos(angles), jnp.sin(angles)
        rot = [a * cosine - b * sine, a * sine + b * cosine]
        own = jnp.concatenate([lat] + rot * (LANES // rope), axis=1).astype(jnp.bfloat16)
        keys_in = lax.all_gather(own, ("blk", "head"), axis=0, tiled=True)
    any_space = pl.BlockSpec(memory_space=pl.ANY)
    vmem = pl.BlockSpec(memory_space=pltpu.VMEM)
    dims = (tokens, heads, nope, latent, rope, value, total, slices)
    return pl.pallas_call(
        functools.partial(body, dims, remote),
        out_shape=jax.ShapeDtypeStruct((tokens, heads * value), jnp.bfloat16),
        in_specs=[
            pl.BlockSpec(memory_space=pltpu.SMEM),
            vmem if remote else any_space,
            vmem,
            vmem,
            any_space,
            any_space,
            any_space,
            any_space,
        ],
        out_specs=any_space,
        scratch_shapes=[
            pltpu.VMEM(query_nope.shape, jnp.bfloat16),
            pltpu.VMEM(query_rope.shape, jnp.bfloat16),
            pltpu.VMEM(key_up.shape, jnp.bfloat16),
            pltpu.VMEM(value_up.shape, jnp.bfloat16),
            pltpu.VMEM((tokens, heads * value), jnp.bfloat16),
            pltpu.VMEM((total, latent + LANES), jnp.bfloat16),
            pltpu.VMEM((heads * tokens, latent + LANES), jnp.bfloat16),
            pltpu.VMEM((tokens, total), jnp.float32),
            pltpu.SemaphoreType.DMA((5,)),
            pltpu.SemaphoreType.DMA((1,)),
            pltpu.SemaphoreType.DMA((2 * blocks if remote else 1,)),
            pltpu.SemaphoreType.DMA((2 * blocks if remote else 1,)),
        ],
        compiler_params=pltpu.CompilerParams(
            vmem_limit_bytes=60 * 1024 * 1024,
            has_side_effects=remote,
            **({"collective_id": 0} if remote else {}),
        ),
    )(span_order, keys_in, gain, freq, query_nope, query_rope, key_up, value_up)


def solution(mesh):
    in_specs = (
        P("blk", "head"),
        P("blk", "head"),
        P(("blk", "head"), None),
        P(),
        P("head", None, None),
        P("head", None, None),
        P(),
    )
    return jax.shard_map(
        functools.partial(shards, mesh),
        mesh=mesh,
        in_specs=in_specs,
        out_specs=P("blk", "head"),
        check_vma=False,
    )
```

profile of v0, /device:TPU:1, one launch (start us, length us, event | category | flops | bytes accessed | tf_op | source)
XLA Modules:
  0.0 29.2 jit_solution(5748279849860432951)
XLA Ops:
  0.0 27.4 %shard_map.82 = bf16[64,4096]{1,0:T(8,128)(2,1)} custom-call(s32[32]{0:T(128)} %span_ref.1, bf16[32,576]{1,0:T(8,128)(2,1)} %keys_in_ref.1, f32[1,512]{1,0:T(1,128)} %bitcast.1, f32[1,128]{1,0:T(1,128)} %constant.3.freq_ref, bf16[64,4096]{1,0:T(8,128)(2,1)} %nope_hbm.1, bf16[64,2048]{1,0:T(8,128)(2,1)} %rope_hbm.1, bf16[32,128,512]{2,1,0:T(8,128)(2,1)} %key_up_hbm.1, ...), custom_call_target="tpu_custom_call" | custom-call | tf_op jit(solution)/shard_map/pallas_call | solution.py:300
  27.4 1.9 %copy.10 = bf16[64,4096]{1,0:T(8,128)(2,1)} copy(bf16[64,4096]{1,0:T(8,128)(2,1)} %shard_map.82) | data formatting | bytes 1048576
where the time goes:
time: 29.5 us; the launch traced here: 29.2 us
  Pallas kernels  27.4 us (93%)
  local copies, waits for them, and re-layouts  1.87 us (6%)
    pallas_call x1, Pallas kernels, shards(): pl.pallas_call(functools.partial(body, dims, remote), out_shape=jax.Shape...  27.4 us
    unnamed x1, local copies, waits for them, and re-layouts  1.87 us

commit v1 on v0

--- a/solution.py
+++ b/solution.py
@@ -13,7 +13,9 @@
 rope_base = 10000.0
 masked_score = -1e30
 LANES = 128
-GROUP = 16
+GROUP = 8
+LAG = 1
+CHUNK = 256
 MESH = pl.DeviceIdType.MESH
 
 
@@ -47,34 +49,34 @@
     rope_hbm,
     key_up_hbm,
     value_up_hbm,
-    out_hbm,
+    out_ref,
     nope_ref,
     rope_ref,
     key_up_ref,
     value_up_ref,
-    out_ref,
     keys_ref,
     query_ref,
     mask_ref,
+    acc_ref,
+    top_ref,
+    sum_ref,
     load_sem,
-    out_sem,
     send_sem,
     recv_sem,
+    ready_sem,
 ):
-    tokens, heads, nope, latent, rope, value, total, slices = dims
+    tokens, heads, nope, latent, rope, value, total, slices, chunk = dims
     half_block = tokens // 2
     scale = (nope + rope) ** (-0.5) * math.log2(math.e)
     blk = lax.axis_index("blk")
     head = lax.axis_index("head")
+    chunks = total // chunk
     loads = [
         pltpu.make_async_copy(nope_hbm, nope_ref, load_sem.at[0]),
         pltpu.make_async_copy(rope_hbm, rope_ref, load_sem.at[1]),
         pltpu.make_async_copy(key_up_hbm, key_up_ref, load_sem.at[2]),
         pltpu.make_async_copy(value_up_hbm, value_up_ref, load_sem.at[3]),
     ]
-    for load in loads:
-        load.start()
-
     sends = []
     if remote:
         outer = lax.axis_size("blk") // 4
@@ -89,7 +91,7 @@
         def block_at(index):
             return keys_ref.at[pl.ds(pl.multiple_of(index * slices, slices), slices)]
 
-        def send(index, target):
+        def copy_to(index, target):
             copy = pltpu.make_async_remote_copy(
                 src_ref=block_at(index),
                 dst_ref=block_at(index),
@@ -98,8 +100,8 @@
                 device_id=target,
                 device_id_type=MESH,
             )
-            copy.start()
             sends.append(copy)
+            return copy
 
         def arrive(index):
             pltpu.make_async_remote_copy(
@@ -107,25 +109,32 @@
                 dst_ref=block_at(index),
                 send_sem=send_sem.at[0],
                 recv_sem=recv_sem.at[index],
-                device_id=device(o, i, 1 - c, head),
+                device_id=sibling,
                 device_id_type=MESH,
             ).wait_recv()
 
+        def plane(k):
+            return (k - 1) + ((k - 1) - o + outer) // outer
+
         sibling = device(o, i, 1 - c, head)
-        i_peer = device(o, 1 - i, c, head)
-        h_peer = device(o, i, c, 1 - head)
-        order = []
-        for d in range(1, outer // 2 + 1):
-            order.append(d)
-            if d != outer - d:
-                order.append(outer - d)
-        at = lambda d: lax.rem(o + d, outer)
-        o_peers = [device(at(d), i, c, head) for d in order]
-        peers = [sibling, i_peer, h_peer] + o_peers
+        corners = [(1 - i, 1 - head), (i, 1 - head), (1 - i, head)]
+        flat = [device(o, i_, c, h_) for i_, h_ in corners]
+        partners = [
+            (device(plane(k), i, c, head), plane(k), o, plane(k) < o) for k in range(1, outer)
+        ]
+        for n, (peer, low) in enumerate(zip(flat + [sibling], (i == 1, head == 1, i == 1, c == 0))):
+            partners.append((peer, outer + n, outer + n, low))
         barrier = pltpu.get_barrier_semaphore()
-        for peer in peers:
-            pl.semaphore_signal(barrier, inc=1, device_id=peer, device_id_type=MESH)
-
+        for peer, _, _, low in partners:
+
+            @pl.when(jnp.logical_not(low))
+            def _():
+                pl.semaphore_signal(barrier, inc=1, device_id=peer, device_id_type=MESH)
+
+    for load in loads:
+        load.start()
+
+    if remote:
         first_row = blk * tokens + head * slices
         own_pos = (
             span_ref[first_row // half_block] * half_block
@@ -147,9 +156,28 @@
         own_block[:, :latent] = own_latent.astype(jnp.bfloat16)
         own_block[:, latent:] = rotate_tile(own_rope, cosine, sine, rope).astype(jnp.bfloat16)
 
-        pl.semaphore_wait(barrier, len(peers))
-        for peer in [i_peer, h_peer] + o_peers + [sibling]:
-            send(own_slot, peer)
+        ahead = o + head + 2 * i + (1 - c)
+
+        @pl.when(ahead > 0)
+        def _():
+            pl.semaphore_wait(barrier, ahead)
+
+        own_copies = [copy_to(own_slot, peer) for peer, _, _, _ in partners]
+        for (peer, _, there, low), copy in zip(partners, own_copies):
+
+            @pl.when(low)
+            def _():
+                pl.semaphore_signal(ready_sem.at[there], inc=1, device_id=peer, device_id_type=MESH)
+                copy.start()
+
+        def send_own(n):
+            _, here, _, low = partners[n]
+
+            @pl.when(jnp.logical_not(low))
+            def _():
+                pl.semaphore_wait(ready_sem.at[here], 1)
+                own_copies[n].start()
+
     else:
         keys_copy = pltpu.make_async_copy(keys_in_ref, keys_ref, load_sem.at[4])
         keys_copy.start()
@@ -165,8 +193,13 @@
     for entry in range(total // half_block):
         key_span = jnp.where(key_half == entry, span_ref[entry], key_span)
     key_pos = key_span * half_block + key_lane % half_block
-    mask_ref[...] = jnp.where(key_pos[:1] <= query_pos[:, :1], 0.0, masked_score)
+    mask = jnp.where(key_pos[:1] <= query_pos[:, :1], 0.0, masked_score)
+    for n in range(chunks):
+        mask_ref[n] = mask[:, n * chunk : (n + 1) * chunk]
     cosine, sine = angles_of(query_pos, freq_ref[...], rope)
+    if remote:
+        for n in (outer + 2, outer, outer + 1, outer - 1):
+            send_own(n)
     loads[1].wait()
     per_tile = LANES // rope
     lane = lax.broadcasted_iota(jnp.int32, (tokens, LANES), 1)
@@ -180,86 +213,121 @@
             ).astype(jnp.bfloat16)
 
     if remote:
-        for d in order:
-            index = slot(at(d), i, c, head)
-            arrive(index)
-            for peer in (i_peer, h_peer, sibling):
-                send(index, peer)
-
+        for k in range(1, outer):
+            send_own(k - 1)
     loads[0].wait()
     loads[2].wait()
-
-    def lift(first, count):
-        for h in range(first, first + count):
-            query_ref[h * tokens : (h + 1) * tokens, :latent] = jnp.dot(
-                nope_ref[:, h * nope : (h + 1) * nope],
-                key_up_ref[h],
-                preferred_element_type=jnp.float32,
-            ).astype(jnp.bfloat16)
-
-    if remote:
-        steps = [0] + order
-        per_step = -(-heads // len(steps))
-        for n, d in enumerate(steps):
-            lift(n * per_step, max(0, min(per_step, heads - n * per_step)))
-            via_h, via_i = slot(at(d), i, c, 1 - head), slot(at(d), 1 - i, c, head)
-            arrive(via_i)
-            if d % 2 == 1:
-                send(via_i, h_peer)
-            send(via_i, sibling)
-            arrive(via_h)
-            if d % 2 == 0:
-                send(via_h, i_peer)
-            send(via_h, sibling)
-        for d in steps:
-            index = slot(at(d), 1 - i, c, 1 - head)
-            arrive(index)
-            send(index, sibling)
-        for d in steps:
-            for i_ in (i, 1 - i):
-                for h_ in (head, 1 - head):
-                    arrive(slot(at(d), i_, 1 - c, h_))
-    else:
-        lift(0, heads)
-        keys_copy.wait()
-    loads[3].wait()
+    for h in range(heads):
+        query_ref[h * tokens : (h + 1) * tokens, :latent] = jnp.dot(
+            nope_ref[:, h * nope : (h + 1) * nope],
+            key_up_ref[h],
+            preferred_element_type=jnp.float32,
+        ).astype(jnp.bfloat16)
 
     group = min(GROUP, heads)
     rows = group * tokens
 
-    def attend(g, _):
-        start = pl.multiple_of(g * rows, rows)
+    def keys_of(n):
+        return keys_ref.at[pl.ds(pl.multiple_of(n * chunk, chunk), chunk)]
+
+    def scores_of(n, g):
         scores = lax.dot_general(
-            query_ref[pl.ds(start, rows), :],
-            keys_ref[...],
+            query_ref[g * rows : (g + 1) * rows, :],
+            keys_of(n)[...],
             (((1,), (1,)), ((), ())),
             preferred_element_type=jnp.float32,
         )
-        scores = scores.reshape(group, tokens, total) + mask_ref[...][None]
-        top = jnp.max(scores, axis=2, keepdims=True)
-        weight = jnp.exp2((scores - top) * scale)
-        sums = jnp.sum(weight, axis=2, keepdims=True).reshape(rows, 1)
+        return (scores.reshape(group, tokens, chunk) + mask_ref[n][None]).reshape(rows, chunk)
+
+    def wide(array, width):
+        return jnp.concatenate([array] * (width // LANES), axis=1)
+
+    def weigh(n, g, scores, first, last):
+        at = slice(g * rows, (g + 1) * rows)
+        top = jnp.broadcast_to(jnp.max(scores, axis=1, keepdims=True), (rows, LANES))
+        if not first:
+            old = top_ref[at]
+            top = jnp.maximum(top, old)
+            fade = jnp.exp2((old - top) * scale)
+        weight = jnp.exp2((scores - wide(top, chunk)) * scale)
+        sums = weight[:, :LANES]
+        for part in range(1, chunk // LANES):
+            sums = sums + weight[:, part * LANES : (part + 1) * LANES]
         product = jnp.dot(
-            weight.reshape(rows, total).astype(jnp.bfloat16),
-            keys_ref[:, :latent],
+            weight.astype(jnp.bfloat16),
+            keys_of(n)[:, :latent],
             preferred_element_type=jnp.float32,
         )
-        lat_out = (product * (1.0 / sums)).astype(jnp.bfloat16)
-        for n in range(group):
-            column = pl.multiple_of((g * group + n) * value, value)
-            out_ref[:, pl.ds(column, value)] = jnp.dot(
-                lat_out[n * tokens : (n + 1) * tokens],
-                value_up_ref[g * group + n],
+        if not first:
+            sums = sums + sum_ref[at] * fade
+            product = product + acc_ref[at] * wide(fade, latent)
+        if not last:
+            top_ref[at] = top
+            sum_ref[at] = sums
+            acc_ref[at] = product
+            return
+        share = 1.0 / jnp.sum(sums, axis=1, keepdims=True)
+        lat_out = (product * share).astype(jnp.bfloat16)
+        for m in range(group):
+            h = g * group + m
+            out_ref[:, h * value : (h + 1) * value] = jnp.dot(
+                lat_out[m * tokens : (m + 1) * tokens],
+                value_up_ref[h],
                 preferred_element_type=jnp.float32,
             ).astype(jnp.bfloat16)
-        return 0
-
-    lax.fori_loop(0, heads // group, attend, 0)
-    store = pltpu.make_async_copy(out_ref, out_hbm, out_sem.at[0])
-    store.start()
-    for copy in sends:
-        copy.wait_send()
-    store.wait()
+
+    def attend(n, first, last):
+        waiting = []
+        for g in range(heads // group):
+            waiting.append((g, scores_of(n, g)))
+            if len(waiting) > LAG:
+                weigh(n, *waiting.pop(0), first, last)
+        for entry in waiting:
+            weigh(n, *entry, first, last)
+
+    if remote:
+        for k in range(1, outer):
+            index = slot(plane(k), i, c, head)
+            arrive(index)
+            for peer in flat + [sibling]:
+                copy_to(index, peer).start()
+
+        def relay(p):
+            for i_, h_ in corners[1:] + corners[:1]:
+                index = slot(p, i_, c, h_)
+                arrive(index)
+                copy_to(index, sibling).start()
+
+        def settle(p):
+            for i_, h_ in [(i, head)] + corners[1:] + corners[:1]:
+                arrive(slot(p, i_, 1 - c, h_))
+
+        order = [o] + [plane(k) for k in range(1, outer)]
+        relay(order[0])
+        for n, p in enumerate(order):
+            settle(p)
+            last = n == outer - 1
+            if last:
+                loads[3].wait()
+            attend(p, n == 0, last)
+            if not last:
+                relay(order[n + 1])
+        for copy in sends:
+            copy.wait_send()
+    else:
+        keys_copy.wait()
+        loads[3].wait()
+        if chunks == 1:
+            attend(0, True, True)
+        else:
+            attend(0, True, False)
+
+            def step(n, _):
+                attend(n, False, False)
+                return 0
+
+            lax.fori_loop(1, chunks - 1, step, 0)
+            attend(chunks - 1, False, True)
 
 
 def shards(
@@ -295,11 +363,13 @@
         own = jnp.concatenate([lat] + rot * (LANES // rope), axis=1).astype(jnp.bfloat16)
         keys_in = lax.all_gather(own, ("blk", "head"), axis=0, tiled=True)
     any_space = pl.BlockSpec(memory_space=pl.ANY)
+    rows = heads * tokens
+    chunk = total // (blocks // 4) if remote else min(CHUNK, total)
     vmem = pl.BlockSpec(memory_space=pltpu.VMEM)
-    dims = (tokens, heads, nope, latent, rope, value, total, slices)
+    dims = (tokens, heads, nope, latent, rope, value, total, slices, chunk)
     return pl.pallas_call(
         functools.partial(body, dims, remote),
-        out_shape=jax.ShapeDtypeStruct((tokens, heads * value), jnp.bfloat16),
+        out_shape=pltpu.VMEM((tokens, heads * value), jnp.bfloat16),
         in_specs=[
             pl.BlockSpec(memory_space=pltpu.SMEM),
             vmem if remote else any_space,
@@ -310,20 +380,22 @@
             any_space,
             any_space,
         ],
-        out_specs=any_space,
+        out_specs=vmem,
         scratch_shapes=[
             pltpu.VMEM(query_nope.shape, jnp.bfloat16),
             pltpu.VMEM(query_rope.shape, jnp.bfloat16),
             pltpu.VMEM(key_up.shape, jnp.bfloat16),
             pltpu.VMEM(value_up.shape, jnp.bfloat16),
-            pltpu.VMEM((tokens, heads * value), jnp.bfloat16),
             pltpu.VMEM((total, latent + LANES), jnp.bfloat16),
-            pltpu.VMEM((heads * tokens, latent + LANES), jnp.bfloat16),
-            pltpu.VMEM((tokens, total), jnp.float32),
+            pltpu.VMEM((rows, latent + LANES), jnp.bfloat16),
+            pltpu.VMEM((total // chunk, tokens, chunk), jnp.float32),
+            pltpu.VMEM((rows, latent), jnp.float32),
+            pltpu.VMEM((rows, LANES), jnp.float32),
+            pltpu.VMEM((rows, LANES), jnp.float32),
             pltpu.SemaphoreType.DMA((5,)),
-            pltpu.SemaphoreType.DMA((1,)),
             pltpu.SemaphoreType.DMA((2 * blocks if remote else 1,)),
             pltpu.SemaphoreType.DMA((2 * blocks if remote else 1,)),
+            pltpu.SemaphoreType.REGULAR((blocks // 4 + 4,)),
         ],
         compiler_params=pltpu.CompilerParams(
             vmem_limit_bytes=60 * 1024 * 1024,

time: 29.5 us -> 24.4 us (0.83)
  the two profiles are of different devices: /device:TPU:1 before, /device:TPU:25 now
where the time goes in v1:
time: 24.4 us; the launch traced here: 24.2 us
  Pallas kernels  23.4 us (96%)
  local copies, waits for them, and re-layouts  0.8 us (3%)
    pallas_call x1, Pallas kernels, shards(): pl.pallas_call(functools.partial(body, dims, remote), out_shape=pltpu.VME...  23.4 us
    unnamed x1, local copies, waits for them, and re-layouts  0.8 us

profile of v1, /device:TPU:25, one launch (start us, length us, event | category | flops | bytes accessed | tf_op | source)
XLA Modules:
  0.0 24.2 jit_solution(5845648486885151715)
XLA Ops:
  0.0 23.4 %shard_map.82 = bf16[64,4096]{1,0:T(8,128)(2,1)S(1)} custom-call(s32[32]{0:T(128)} %span_ref.1, bf16[32,576]{1,0:T(8,128)(2,1)} %keys_in_ref.1, f32[1,512]{1,0:T(1,128)} %bitcast.1, f32[1,128]{1,0:T(1,128)} %constant.3.freq_ref, bf16[64,4096]{1,0:T(8,128)(2,1)} %nope_hbm.1, bf16[64,2048]{1,0:T(8,128)(2,1)} %rope_hbm.1, bf16[32,128,512]{2,1,0:T(8,128)(2,1)} %key_up_hbm.1, ...), custom_call_target="tpu_custom_call" | custom-call | tf_op jit(solution)/shard_map/pallas_call | solution.py:370
  23.4 0.8 %copy.10 = bf16[64,4096]{1,0:T(8,128)(2,1)} copy(bf16[64,4096]{1,0:T(8,128)(2,1)S(1)} %shard_map.82) | data formatting | bytes 1048576

commit v2 on v1

v2 whole, which is shorter than its diff:
```python
import functools
import math

import jax
import jax.numpy as jnp
import numpy as np
from jax import lax
from jax.experimental import pallas as pl
from jax.experimental.pallas import tpu as pltpu
from jax.sharding import PartitionSpec as P

norm_epsilon = 1e-06
rope_base = 10000.0
masked_score = -1e30
LANES = 128
GROUP = 8
LAG = 1
CHUNK = 256
MESH = pl.DeviceIdType.MESH


def rotate_tile(tile, cosine, signed_sine, rope_width):
    half = rope_width // 2
    width = tile.shape[-1]
    lane = lax.broadcasted_iota(jnp.int32, tile.shape, 1)
    partner = jnp.where(
        lane % rope_width < half,
        pltpu.roll(tile, width - half, 1),
        pltpu.roll(tile, half, 1),
    )
    return tile * cosine + partner * signed_sine


def angles_of(positions, freq, rope_width):
    angles = positions.astype(jnp.float32) * freq
    lane = lax.broadcasted_iota(jnp.int32, angles.shape, 1)
    sine = jnp.sin(angles)
    return jnp.cos(angles), jnp.where(lane % rope_width < rope_width // 2, -sine, sine)


def body(
    dims,
    remote,
    span_hbm,
    keys_in_hbm,
    gain_hbm,
    freq_hbm,
    nope_hbm,
    rope_hbm,
    key_up_hbm,
    value_up_hbm,
    out_ref,
    span_ref,
    keys_in_ref,
    gain_ref,
    freq_ref,
    nope_ref,
    rope_ref,
    key_up_ref,
    value_up_ref,
    wire_ref,
    keys_ref,
    query_ref,
    mask_ref,
    acc_ref,
    top_ref,
    sum_ref,
    part_ref,
    score_ref,
    load_sem,
    send_sem,
    recv_sem,
    ready_sem,
):
    tokens, heads, nope, latent, rope, value, total, slices, width = dims
    half_block = tokens // 2
    scale = (nope + rope) ** (-0.5) * math.log2(math.e)
    blk = lax.axis_index("blk")
    head = lax.axis_index("head")
    fields = total // width
    loads = [
        pltpu.make_async_copy(nope_hbm, nope_ref, load_sem.at[0]),
        pltpu.make_async_copy(rope_hbm, rope_ref, load_sem.at[1]),
        pltpu.make_async_copy(key_up_hbm, key_up_ref, load_sem.at[2]),
        pltpu.make_async_copy(value_up_hbm, value_up_ref, load_sem.at[3]),
    ]
    small = [
        pltpu.make_async_copy(span_hbm, span_ref, load_sem.at[5]),
        pltpu.make_async_copy(freq_hbm, freq_ref, load_sem.at[6]),
        pltpu.make_async_copy(gain_hbm, gain_ref, load_sem.at[7]),
    ]
    if remote:
        small.append(pltpu.make_async_copy(keys_in_hbm, keys_in_ref, load_sem.at[4]))
    sends = []
    if remote:
        outer = lax.axis_size("blk") // 4
        o, i, c = blk // 4, (blk // 2) % 2, blk % 2

        def device(o_, i_, c_, h_):
            return ((o_ * 2 + i_) * 2 + c_, h_)

        tiles = latent // LANES
        packed = slices * tiles + slices // 2
        def slot(o_, i_, c_, h_):
            return ((c_ * outer + o_) * 2 + i_) * 2 + h_

        def block_at(index):
            return wire_ref.at[pl.ds(pl.multiple_of(index * packed, 16), packed)]

        def line_of(p):
            return p

        def corner_of(p):
            return outer + p

        def sibling_of(p):
            return 2 * outer + p

        diagonal = 3 * outer
        counts = [0]

        def copy_to(index, target, landing, when=None):
            copy = pltpu.make_async_remote_copy(
                src_ref=block_at(index),
                dst_ref=block_at(index),
                send_sem=send_sem.at[0 if when is None else 1],
                recv_sem=recv_sem.at[landing],
                device_id=target,
                device_id_type=MESH,
            )
            if when is None:
                counts[0] += 1
            else:
                pl.when(when)(copy.start)
            return copy

        def arrive(landing, blocks):
            pltpu.make_async_remote_copy(
                src_ref=wire_ref.at[: blocks * packed],
                dst_ref=wire_ref.at[: blocks * packed],
                send_sem=send_sem.at[0],
                recv_sem=recv_sem.at[landing],
                device_id=sibling,
                device_id_type=MESH,
            ).wait_recv()

        def at_least(a, b):
            return (a - b + 2 * outer) // (2 * outer)

        above = outer - 1 - o
        upward = at_least(above, o)
        paired = o * upward + above * (1 - upward)

        def plane(k):
            near = at_least(2 * paired, k)
            by_turns = o - (k + 1) // 2 if k % 2 else o + k // 2
            onward = (o + k - paired) * upward + (o - k + paired) * (1 - upward)
            return by_turns * near + onward * (1 - near)

        sibling = device(o, i, 1 - c, head)
        corners = [(1 - i, 1 - head), (i, 1 - head), (1 - i, head)]
        flat = [device(o, i_, c, h_) for i_, h_ in corners]
        partners = []
        for n, (peer, low) in enumerate(zip(flat + [sibling], (i == 1, head == 1, i == 1, c == 0))):
            partners.append((peer, outer + n, outer + n, low))
        for k in range(1, outer):
            p = plane(k)
            partners.append((device(p, i, c, head), p, o, p < o))
        barrier = pltpu.get_barrier_semaphore()
        for peer, _, _, low in partners:

            @pl.when(jnp.logical_not(low))
            def _():
                pl.semaphore_signal(barrier, inc=1, device_id=peer, device_id_type=MESH)

    for load in small + loads:
        load.start()

    if remote:
        ahead = o + head + 2 * i + (1 - c)

        @pl.when(ahead > 0)
        def _():
            pl.semaphore_wait(barrier, ahead)

        for peer, _, there, low in partners:

            @pl.when(low)
            def _():
                pl.semaphore_signal(ready_sem.at[there], inc=1, device_id=peer, device_id_type=MESH)

        for load in small:
            load.wait()
        first_row = blk * tokens + head * slices
        own_pos = (
            span_ref[first_row // half_block] * half_block
            + first_row % half_block
            + lax.broadcasted_iota(jnp.int32, (slices, LANES), 0)
        )
        own = keys_in_ref[...].astype(jnp.float32)
        own_latent = own[:, :latent]
        own_latent = (
            own_latent
            * lax.rsqrt(jnp.mean(own_latent * own_latent, axis=1, keepdims=True) + norm_epsilon)
            * gain_ref[...]
        )
        cosine, sine = angles_of(own_pos, freq_ref[...], rope)
        own_rope = own[:, latent : latent + rope]
        own_rope = jnp.concatenate([own_rope] * (LANES // rope), axis=1)
        own_slot = slot(o, i, c, head)
        own_block = block_at(own_slot)
        for n in range(tiles):
            own_block[n * slices : (n + 1) * slices] = own_latent[
                :, n * LANES : (n + 1) * LANES
            ].astype(jnp.bfloat16)
        rotated = rotate_tile(own_rope, cosine, sine, rope)
        left = lax.broadcasted_iota(jnp.int32, (slices // 2, LANES), 1) < rope
        own_block[slices * tiles :] = jnp.where(
            left, rotated[: slices // 2], rotated[slices // 2 :]
        ).astype(jnp.bfloat16)

        def unpack(p):
            for c_ in range(2):
                for n in range(4):
                    index = (c_ * outer + p) * 4 + n
                    block = block_at(index)
                    row = pl.multiple_of(index * slices, slices)
                    for m in range(tiles):
                        keys_ref[pl.ds(row, slices), m * LANES : (m + 1) * LANES] = block[
                            m * slices : (m + 1) * slices
                        ]
                    pair = block[slices * tiles :].astype(jnp.float32)
                    turned = pltpu.roll(pair, rope, 1)
                    keys_ref[pl.ds(row, slices), latent:] = jnp.concatenate(
                        [jnp.where(left, pair, turned), jnp.where(left, turned, pair)], axis=0
                    ).astype(jnp.bfloat16)


        landings = [diagonal, corner_of(o), corner_of(o), sibling_of(o)] + [line_of(o)] * (outer - 1)
        own_copies = [
            copy_to(own_slot, peer, landing)
            for (peer, _, _, _), landing in zip(partners, landings)
        ]
        for (_, _, _, low), copy in reversed(list(zip(partners, own_copies))):
            pl.when(low)(copy.start)

        def send_own(n):
            _, here, _, low = partners[n]

            @pl.when(jnp.logical_not(low))
            def _():
                pl.semaphore_wait(ready_sem.at[here], 1)
                own_copies[n].start()

    else:
        for load in small:
            load.wait()
        keys_copy = pltpu.make_async_copy(keys_in_hbm, keys_ref, load_sem.at[4])
        keys_copy.start()

    token = lax.broadcasted_iota(jnp.int32, (tokens, LANES), 0)
    query_pos = (
        jnp.where(token < half_block, span_ref[blk * 2], span_ref[blk * 2 + 1]) * half_block
        + token % half_block
    )
    key_lane = lax.broadcasted_iota(jnp.int32, (8, total), 1)
    if remote:
        index = key_lane // slices
        key_row = (((index // 4) % outer * 2 + (index // 2) % 2) * 2 + index // (4 * outer)) * 2
        key_row = (key_row + index % 2) * slices + key_lane % slices
    else:
        key_row = key_lane
    key_half = key_row // half_block
    key_span = jnp.zeros((8, total), jnp.int32)
    for entry in range(total // half_block):
        key_span = jnp.where(key_half == entry, span_ref[entry], key_span)
    key_pos = key_span * half_block + key_row % half_block
    mask = jnp.where(key_pos[:1] <= query_pos[:, :1], 0.0, masked_score)
    for n in range(fields):
        mask_ref[n] = mask[:, n * width : (n + 1) * width]
    cosine, sine = angles_of(query_pos, freq_ref[...], rope)
    if remote:
        for n in (3, 1, 2, 0):
            send_own(n)
    loads[1].wait()
    per_tile = LANES // rope
    lane = lax.broadcasted_iota(jnp.int32, (tokens, LANES), 1)
    for tile in range(heads // per_tile):
        columns = rope_ref[:, tile * LANES : (tile + 1) * LANES].astype(jnp.float32)
        rotated = rotate_tile(columns, cosine, sine, rope)
        for part in range(per_tile):
            row = (tile * per_tile + part) * tokens
            query_ref[row : row + tokens, latent:] = jnp.where(
                lane // rope == part, rotated, 0.0
            ).astype(jnp.bfloat16)

    loads[0].wait()
    loads[2].wait()
    for h in range(heads):
        query_ref[h * tokens : (h + 1) * tokens, :latent] = jnp.dot(
            nope_ref[:, h * nope : (h + 1) * nope],
            key_up_ref[h],
            preferred_element_type=jnp.float32,
        ).astype(jnp.bfloat16)

    group = min(GROUP, heads)
    rows = group * tokens

    def keys_of(chunk, columns=latent + LANES):
        return jnp.concatenate(
            [
                keys_ref[pl.ds(pl.multiple_of(n * width, width), width), :columns]
                for n in chunk
            ],
            axis=0,
        )

    def scores_of(chunk, g):
        scores = lax.dot_general(
            query_ref[g * rows : (g + 1) * rows, :],
            keys_of(chunk),
            (((1,), (1,)), ((), ())),
            preferred_element_type=jnp.float32,
        )
        mask = jnp.concatenate([mask_ref[n] for n in chunk], axis=1)
        return (scores.reshape(group, tokens, -1) + mask[None]).reshape(rows, -1)

    def wide(array, columns):
        return jnp.concatenate([array] * (columns // LANES), axis=1)

    def finish(g, product, sums):
        share = 1.0 / jnp.sum(sums, axis=1, keepdims=True)
        lat_out = (product * share).astype(jnp.bfloat16)
        for m in range(group):
            h = g * group + m
            out_ref[:, h * value : (h + 1) * value] = jnp.dot(
                lat_out[m * tokens : (m + 1) * tokens],
                value_up_ref[h],
                preferred_element_type=jnp.float32,
            ).astype(jnp.bfloat16)

    def weigh(chunk, g, scores, first, last):
        keys = len(chunk) * width
        at = slice(g * rows, (g + 1) * rows)
        top = jnp.broadcast_to(jnp.max(scores, axis=1, keepdims=True), (rows, LANES))
        if not first:
            old = top_ref[at]
            top = jnp.maximum(top, old)
            fade = jnp.exp2((old - top) * scale)
        weight = jnp.exp2((scores - wide(top, keys)) * scale)
        sums = weight[:, :LANES]
        for part in range(1, keys // LANES):
            sums = sums + weight[:, part * LANES : (part + 1) * LANES]
        product = jnp.dot(
            weight.astype(jnp.bfloat16),
            keys_of(chunk, latent),
            preferred_element_type=jnp.float32,
        )
        if not first:
            sums = sums + sum_ref[at] * fade
            product = product + acc_ref[at] * wide(fade, latent)
        if not last:
            top_ref[at] = top
            sum_ref[at] = sums
            acc_ref[at] = product
            return
        finish(g, product, sums)

    def collect(chunk, at):
        for g in range(heads // group):
            scores = scores_of(chunk, g)
            where = slice(g * rows, (g + 1) * rows)
            score_ref[at, where] = scores
            part = part_ref[where] if at else top_ref[where]
            for n in range(len(chunk) * width // LANES):
                part = jnp.maximum(part, scores[:, n * LANES : (n + 1) * LANES])
            part_ref[where] = part

    def conclude(chunks):
        keys = sum(len(chunk) for chunk in chunks) * width
        values = [n for chunk in chunks for n in chunk]

        def weights(g):
            where = slice(g * rows, (g + 1) * rows)
            top = jnp.max(part_ref[where], axis=1, keepdims=True)
            top = jnp.broadcast_to(top, (rows, LANES))
            fade = jnp.exp2((top_ref[where] - top) * scale)
            scores = jnp.concatenate([score_ref[n, where] for n in range(len(chunks))], axis=1)
            weight = jnp.exp2((scores - wide(top, keys)) * scale)
            sums = sum_ref[where] * fade
            for n in range(keys // LANES):
                sums = sums + weight[:, n * LANES : (n + 1) * LANES]
            return g, weight.astype(jnp.bfloat16), fade, sums

        def close(g, weight, fade, sums):
            where = slice(g * rows, (g + 1) * rows)
            product = jnp.dot(weight, keys_of(values, latent), preferred_element_type=jnp.float32)
            finish(g, product + acc_ref[where] * wide(fade, latent), sums)

        ready = weights(0)
        for g in range(1, heads // group):
            following = weights(g)
            close(*ready)
            ready = following
        close(*ready)

    def attend(chunk, first, last, low=0, high=heads // group):
        waiting = []
        for g in range(low, high):
            waiting.append((g, scores_of(chunk, g)))
            if len(waiting) > LAG:
                weigh(chunk, *waiting.pop(0), first, last)
        for entry in waiting:
            weigh(chunk, *entry, first, last)

    if remote:

        def forward(p):
            index = slot(p, i, c, head)
            arrive(line_of(p), 1)
            for peer in flat[1:3]:
                copy_to(index, peer, corner_of(p)).start()
            copy_to(index, flat[0], corner_of(p), p < o - 1)
            copy_to(index, sibling, sibling_of(p)).start()

        def relay(p, at):
            arrive(corner_of(p), len(at))
            for i_, h_ in at:
                copy_to(slot(p, i_, c, h_), sibling, sibling_of(p)).start()

        half = heads // group // 2
        order = [o] + [plane(k) for k in range(1, outer)]
        others = order[1:]
        for n in range(4, len(partners)):
            send_own(n)
        across = slot(o, 1 - i, c, 1 - head)
        arrive(diagonal, 1)
        for p, (peer, _, _, _) in reversed(list(zip(others, partners[4:]))):
            copy_to(across, peer, corner_of(o), p < o + 2)
        copy_to(across, sibling, sibling_of(o)).start()
        relay(o, corners[1:])
        forward(others[0])
        arrive(sibling_of(o), 4)
        unpack(o)
        attend([o, outer + o], True, False, 0, half)
        for p in others[1:-1]:
            forward(p)
        attend([o, outer + o], True, False, half)
        forward(others[-1])

        numbers = [[p, outer + p] for p in others]
        relay(others[0], corners)
        arrive(sibling_of(others[0]), 4)
        unpack(others[0])
        collect(numbers[0], 0)
        for n in range(1, outer - 1):
            for p in others[1:3] if n == 1 else others[n + 1 : n + 2]:
                relay(p, corners)
            arrive(sibling_of(others[n]), 4)
            unpack(others[n])
            collect(numbers[n], n)
        loads[3].wait()
        conclude(numbers)

        def sent(blocks, at):
            pltpu.make_async_remote_copy(
                src_ref=wire_ref.at[: blocks * packed],
                dst_ref=wire_ref.at[: blocks * packed],
                send_sem=send_sem.at[at],
                recv_sem=recv_sem.at[0],
                device_id=sibling,
                device_id_type=MESH,
            ).wait_send()

        sent(counts[0], 0)
        for n in range(outer):
            taken = n + (n < outer - 1) + max(n - 1, 0)
            pl.when(o == n)(functools.partial(sent, taken, 1))
    else:
        keys_copy.wait()
        loads[3].wait()
        if fields == 1:
            attend([0], True, True)
        else:
            attend([0], True, False)

            def step(n, _):
                attend([n], False, False)
                return 0

            lax.fori_loop(1, fields - 1, step, 0)
            attend([fields - 1], False, True)


def shards(
    mesh, query_nope, query_rope, compressed, latent_gain, key_up, value_up, span_order
):
    tokens, (heads, nope, latent) = query_nope.shape[0], key_up.shape
    rope, value = query_rope.shape[1] // heads, value_up.shape[2]
    slices = compressed.shape[0]
    blocks, head_parts = mesh.shape["blk"], mesh.shape["head"]
    total = blocks * tokens
    half_block = tokens // 2
    half = rope // 2
    remote = head_parts == 2 and blocks % 4 == 0 and blocks >= 16 and slices % 32 == 0 and half_block % slices == 0 and 2 * rope == LANES
    exponents = np.arange(LANES) % half
    freq = jnp.asarray((rope_base ** (-exponents / half)).astype(np.float32))[None]
    gain = latent_gain[None]
    if remote:
        keys_in = compressed
    else:
        rows = (
            lax.axis_index("blk") * tokens
            + lax.axis_index("head") * slices
            + jnp.arange(slices, dtype=jnp.int32)
        )
        pos = span_order[rows // half_block] * half_block + rows % half_block
        wide = compressed.astype(jnp.float32)
        lat = wide[:, :latent]
        lat = lat * lax.rsqrt(jnp.mean(lat * lat, axis=1, keepdims=True) + norm_epsilon) * gain
        angles = pos.astype(jnp.float32)[:, None] * freq[:, :half]
        a, b = wide[:, latent : latent + half], wide[:, latent + half :]
        cosine, sine = jnp.cos(angles), jnp.sin(angles)
        rot = [a * cosine - b * sine, a * sine + b * cosine]
        own = jnp.concatenate([lat] + rot * (LANES // rope), axis=1).astype(jnp.bfloat16)
        keys_in = lax.all_gather(own, ("blk", "head"), axis=0, tiled=True)
    any_space = pl.BlockSpec(memory_space=pl.ANY)
    rows = heads * tokens
    wire_rows = 2 * blocks * slices * (2 * latent + LANES) // (2 * LANES) if remote else 16
    width = 4 * slices if remote else min(CHUNK, total)
    vmem = pl.BlockSpec(memory_space=pltpu.VMEM)
    dims = (tokens, heads, nope, latent, rope, value, total, slices, width)
    return pl.pallas_call(
        functools.partial(body, dims, remote),
        out_shape=pltpu.VMEM((tokens, heads * value), jnp.bfloat16),
        in_specs=[
            any_space,
            any_space,
            any_space,
            any_space,
            any_space,
            any_space,
            any_space,
            any_space,
        ],
        out_specs=vmem,
        scratch_shapes=[
            pltpu.SMEM(span_order.shape, jnp.int32),
            pltpu.VMEM(compressed.shape, jnp.bfloat16),
            pltpu.VMEM(gain.shape, jnp.float32),
            pltpu.VMEM(freq.shape, jnp.float32),
            pltpu.VMEM(query_nope.shape, jnp.bfloat16),
            pltpu.VMEM(query_rope.shape, jnp.bfloat16),
            pltpu.VMEM(key_up.shape, jnp.bfloat16),
            pltpu.VMEM(value_up.shape, jnp.bfloat16),
            pltpu.VMEM((wire_rows, LANES), jnp.bfloat16),
            pltpu.VMEM((total, latent + LANES), jnp.bfloat16),
            pltpu.VMEM((rows, latent + LANES), jnp.bfloat16),
            pltpu.VMEM((total // width, tokens, width), jnp.float32),
            pltpu.VMEM((rows, latent), jnp.float32),
            pltpu.VMEM((rows, LANES), jnp.float32),
            pltpu.VMEM((rows, LANES), jnp.float32),
            pltpu.VMEM((rows, LANES), jnp.float32),
            pltpu.VMEM((blocks // 4 - 1, rows, 2 * width) if remote else (1, 8, LANES), jnp.float32),
            pltpu.SemaphoreType.DMA((8,)),
            pltpu.SemaphoreType.DMA((2,)),
            pltpu.SemaphoreType.DMA((3 * (blocks // 4) + 1 if remote else 1,)),
            pltpu.SemaphoreType.REGULAR((blocks // 4 + 4,)),
        ],
        compiler_params=pltpu.CompilerParams(
            vmem_limit_bytes=60 * 1024 * 1024,
            has_side_effects=remote,
            **({"collective_id": 0} if remote else {}),
        ),
    )(span_order, keys_in, gain, freq, query_nope, query_rope, key_up, value_up)


def solution(mesh):
    in_specs = (
        P("blk", "head"),
        P("blk", "head"),
        P(("blk", "head"), None),
        P(),
        P("head", None, None),
        P("head", None, None),
        P(),
    )
    return jax.shard_map(
        functools.partial(shards, mesh),
        mesh=mesh,
        in_specs=in_specs,
        out_specs=P("blk", "head"),
        check_vma=False,
    )
```

time: 24.4 us -> 21.8 us (0.89)
  Pallas kernels: 23.4 us -> 20.9 us
    pallas_call x1, Pallas kernels: 23.4 us -> 20.9 us  [shards(): pl.pallas_call(functools.partial(body, dims, remote), out_shape=pltpu.VME...]
where the time goes in v2:
time: 21.8 us; the launch traced here: 21.7 us
  Pallas kernels  20.9 us (96%)
  local copies, waits for them, and re-layouts  0.8 us (4%)
    pallas_call x1, Pallas kernels, shards(): pl.pallas_call(functools.partial(body, dims, remote), out_shape=pltpu.VME...  20.9 us
    unnamed x1, local copies, waits for them, and re-layouts  0.8 us

profile of v2, /device:TPU:25, one launch (start us, length us, event | category | flops | bytes accessed | tf_op | source)
XLA Modules:
  0.0 21.7 jit_solution(1648705222528390437)
XLA Ops:
  0.0 20.9 %shard_map.82 = bf16[64,4096]{1,0:T(8,128)(2,1)S(1)} custom-call(s32[32]{0:T(128)} %span_hbm.1, bf16[32,576]{1,0:T(8,128)(2,1)} %keys_in_hbm.1, f32[1,512]{1,0:T(1,128)} %bitcast.1, f32[1,128]{1,0:T(1,128)} %constant.3.freq_hbm, bf16[64,4096]{1,0:T(8,128)(2,1)} %nope_hbm.1, bf16[64,2048]{1,0:T(8,128)(2,1)} %rope_hbm.1, bf16[32,128,512]{2,1,0:T(8,128)(2,1)} %key_up_hbm.1, ...), custom_call_target="tpu_custom_call" | custom-call | tf_op jit(solution)/shard_map/pallas_call | solution.py:533
  20.9 0.8 %copy.10 = bf16[64,4096]{1,0:T(8,128)(2,1)} copy(bf16[64,4096]{1,0:T(8,128)(2,1)S(1)} %shard_map.82) | data formatting | bytes 1048576
